TPU v7x, 32 devices: a whole 2x2x4 slice. The times are simulated.
32 devices in a mesh: grp: 4 (over z), ep: 8 (over y, x, core).
Axes of the slice: x: 2, y: 2, z: 4, core: 2. Of those that a mesh axis runs over, the one named last changes fastest.
Arguments:
- hidden: bfloat16 [4, 8, 32, 1024], P('grp', 'ep'), may hold values from -6 to 6
- down_weight: bfloat16 [8, 1024, 4096], P('ep'), may hold values from -0.1875 to 0.1875
- slot_gate: float32 [4, 8, 32], P('grp', 'ep'), may hold values from 0.02 to 0.6
- slot_owner: int32 [4, 8, 32], P('grp', 'ep'), may hold values from 0 to 3
- slot_row: int32 [4, 8, 32], P('grp', 'ep'), may hold values from 0 to 31
- block_count: int32 [4, 8, 8], P('grp', 'ep'), may hold values from 0 to 4, as said below
Outputs:
- mixed: bfloat16 [1024, 4096], P(('grp', 'ep'))
Inputs may be any that keep to these rules, and one draw needn't show every extreme that they name: `block_count`: every device's expert has at least one block with all 4 slots live.
All inputs are finite; a program needn't handle non-finite values.
Results may differ from a plain program's by a relative error of at most 0.009.
Values may be sent and summed in bfloat16 or wider, within the bound.
A program may use at most 64 MiB of HBM per device.

v0:
```python
import jax
import jax.numpy as jnp
from jax import lax
from jax.sharding import PartitionSpec as P

TOK_DEV = 32


def body(hidden, down_weight, slot_gate, slot_owner, slot_row, block_count):
    columns = lax.axis_size("ep")
    slot_total = hidden.shape[2]
    send = slot_total // columns
    product = jnp.dot(hidden[0, 0], down_weight[0], preferred_element_type=jnp.float32)
    within = jnp.arange(slot_total) % send
    limits = jnp.repeat(block_count[0, 0], send)
    live = (within < limits).astype(jnp.float32)
    scaled = (product * (slot_gate[0, 0] * live)[:, None]).astype(jnp.bfloat16)
    local_index = slot_owner[0, 0] * TOK_DEV + slot_row[0, 0]
    arrived, arrived_index = (
        lax.all_to_all(scaled, "ep", split_axis=0, concat_axis=0, tiled=True),
        lax.all_to_all(local_index, "ep", split_axis=0, concat_axis=0, tiled=True),
    )
    wanted = jnp.arange(lax.axis_size("grp") * TOK_DEV)
    table = (wanted[:, None] == arrived_index[None, :]).astype(jnp.bfloat16)
    return lax.psum_scatter(
        jnp.dot(table, arrived, preferred_element_type=jnp.float32).astype(jnp.bfloat16),
        "grp",
        scatter_dimension=0,
        tiled=True,
    )


def solution(mesh):
    in_specs = (
        P("grp", "ep", None, None),
        P("ep", None, None),
        P("grp", "ep", None),
        P("grp", "ep", None),
        P("grp", "ep", None),
        P("grp", "ep", None),
    )
    out_specs = P(("grp", "ep"), None)
    return jax.shard_map(body, mesh=mesh, in_specs=in_specs, out_specs=out_specs, check_vma=False)
```

profile of v0, /device:TPU:0, one launch (start us, length us, event | category | flops | bytes accessed | tf_op | source)
XLA Modules:
  0.0 66.6 jit_solution(8651157808570100972)
XLA Ops:
  6.5 0.0 copy-start
  6.5 0.7 %add_reduce_fusion = s32[32]{0:T(128)S(1)} fusion(s32[1,1,32]{2,1,0:T(1,128)} %param.10, s32[1,1,32]{2,1,0:T(1,128)} %param.9), kind=kLoop, calls=%fused_computation.10 | loop fusion | flops 64 | bytes 384 | tf_op jit(solution)/shard_map/add | solution.py:18
  7.3 0.7 %add.26 = s32[8,4,1]{1,0,2:T(8,128)} reshape(s32[32]{0:T(128)S(1)} %add_reduce_fusion) | data formatting | bytes 256 | tf_op jit(solution)/shard_map/add | solution.py:18
  7.9 5.2 %all-to-all-start = ((s32[8,4,1]{1,2,0:T(1,128)}), s32[8,4,1]{1,2,0:T(1,128)S(1)}, u32[]{:S(2)}, u32[]{:S(2)}) async-start(s32[8,4,1]{1,2,0:T(1,128)} %bitcast), calls=%async_computation | async-start | bytes 8192 | tf_op jit(solution)/shard_map/all_to_all | solution.py:21
  13.1 0.7 %broadcast_in_dim.2 = s32[8,4]{1,0:T(8,128)S(1)} broadcast(s32[8]{0:T(128)} %bitcast.16), dimensions={0} | broadcast | bytes 160 | tf_op jit(solution)/shard_map/broadcast_in_dim | solution.py:15
  13.9 0.1 reshape.51
  13.9 0.7 compare_select_fusion
  14.6 0.0 copy-done
  14.6 4.9 %fusion.5 = bf16[32,4096]{1,0:T(8,128)(2,1)S(1)} fusion(bf16[1,1024,4096]{2,1,0:T(8,128)(2,1)} %param.7, f32[32]{0:T(128)S(1)} %compare_select_fusion, bf16[1,1,32,1024]{3,2,1,0:T(8,128)(2,1)S(1)} %copy-done), kind=kOutput, calls=%fused_computation.4 | convolution fusion | flops 268697600 | bytes 8716416 | tf_op jit(solution)/shard_map/dot_general | solution.py:13
  19.5 0.8 %all_to_all.13 = bf16[8,4,4096]{2,1,0:T(4,128)(2,1)} reshape(bf16[32,4096]{1,0:T(8,128)(2,1)S(1)} %fusion.5) | data formatting | bytes 524288 | tf_op jit(solution)/shard_map/all_to_all | solution.py:20
  20.3 0.0 all-to-all-done
  20.3 4.2 %all-to-all-start.1 = ((bf16[8,4,4096]{2,1,0:T(4,128)(2,1)}), bf16[8,4,4096]{2,1,0:T(4,128)(2,1)S(1)}, u32[]{:S(2)}, u32[]{:S(2)}) async-start(bf16[8,4,4096]{2,1,0:T(4,128)(2,1)} %all_to_all.13), calls=%async_computation.1 | async-start | bytes 524288 | tf_op jit(solution)/shard_map/all_to_all | solution.py:20
  24.6 0.0 reduce-scatter.2.cloned.1.call-start
  24.6 0.6 broadcast.45
  25.2 0.7 %reduce.7 = s32[8,4]{1,0:T(8,128)S(1)} reduce(s32[8,4,1]{1,2,0:T(1,128)S(1)} %all-to-all-done, s32[]{:T(128)} %broadcast.45), dimensions={2}, to_apply=%all_to_all.12.reduce_sub_computation.3 | reduce | bytes 260 | tf_op jit(solution)/shard_map/all_to_all | solution.py:21
  25.9 0.1 eq.18
  26.0 5.5 %all-to-all-done.1 = bf16[8,4,4096]{2,1,0:T(4,128)(2,1)S(1)} async-done(((bf16[8,4,4096]{2,1,0:T(4,128)(2,1)}), bf16[8,4,4096]{2,1,0:T(4,128)(2,1)S(1)}, u32[]{:S(2)}, u32[]{:S(2)}) %all-to-all-start.1) | async-done | bytes 262176 | tf_op jit(solution)/shard_map/all_to_all | solution.py:20
  31.5 0.1 all_to_all.15
  31.5 1.4 %convolution_convert_fusion = bf16[128,4096]{1,0:T(8,128)(2,1)} fusion(bf16[32,4096]{1,0:T(8,128)(2,1)S(1)} %all_to_all.15, s32[32]{0:T(128)S(1)} %eq.18), kind=kOutput, calls=%fused_computation.2 | convolution fusion | flops 34082816 | bytes 1310848 | tf_op jit(solution)/shard_map/dot_general | solution.py:26
  32.9 0.0 reduce-scatter.2.cloned.1.call-update
  33.0 26.8 %reduce-scatter.2.cloned.1.call-done = bf16[32,4096]{1,0:T(8,128)(2,1)} async-done(((bf16[128,4096]{1,0:T(8,128)(2,1)}), bf16[32,4096]{1,0:T(8,128)(2,1)}) %reduce-scatter.2.cloned.1.call-update) | async-done | bytes 262160 | tf_op jit(solution)/shard_map/reduce_scatter | solution.py:25
Async XLA Ops:
  6.5 8.1 %copy-start = (bf16[1,1,32,1024]{3,2,1,0:T(8,128)(2,1)S(1)}, bf16[1,1,32,1024]{3,2,1,0:T(8,128)(2,1)}, u32[]{:S(2)}) copy-start(bf16[1,1,32,1024]{3,2,1,0:T(8,128)(2,1)} %param.6) | copy-start | bytes 196612
  7.9 12.4 %all-to-all-start = ((s32[8,4,1]{1,2,0:T(1,128)}), s32[8,4,1]{1,2,0:T(1,128)S(1)}, u32[]{:S(2)}, u32[]{:S(2)}) async-start(s32[8,4,1]{1,2,0:T(1,128)} %bitcast), calls=%async_computation | async-start | bytes 8192 | tf_op jit(solution)/shard_map/all_to_all | solution.py:21
  20.3 11.1 %all-to-all-start.1 = ((bf16[8,4,4096]{2,1,0:T(4,128)(2,1)}), bf16[8,4,4096]{2,1,0:T(4,128)(2,1)S(1)}, u32[]{:S(2)}, u32[]{:S(2)}) async-start(bf16[8,4,4096]{2,1,0:T(4,128)(2,1)} %all_to_all.13), calls=%async_computation.1 | async-start | bytes 524288 | tf_op jit(solution)/shard_map/all_to_all | solution.py:20
  24.6 35.2 %reduce-scatter.2.cloned.1.call-start = ((), (), s32[]{:S(2)}) async-start(), calls=%async_computation.3 | async-start | bytes 1310720 | tf_op jit(solution)/shard_map/reduce_scatter | solution.py:25
Sparse Core Ops, SparseCore 0:
  33.1 26.6 reduce-scatter.1
where the time goes:
time: 67 us; the launch traced here: 66.6 us
  waiting for transfers between devices  32.3 us (48%)
  between operations  13.4 us (20%)
  starting transfers between devices  9.44 us (14%)
  matrix products  6.33 us (9%)
  local copies, waits for them, and re-layouts  3.03 us (5%)
  other arithmetic  2.09 us (3%)
    reduce_scatter x1, waiting for transfers between devices, body(): lax.psum_scatter(jnp.dot(table, arrived, preferred_element_type=jnp.float...  26.8 us
    all_to_all x1, waiting for transfers between devices, body(): lax.all_to_all(scaled, 'ep', split_axis=0, concat_axis=0, tiled=True)  5.48 us
    all_to_all x1, starting transfers between devices, body(): lax.all_to_all(local_index, 'ep', split_axis=0, concat_axis=0, tiled=True)  5.2 us
    dot_general x1, matrix products, body(): jnp.dot(hidden[0, 0], down_weight[0], preferred_element_type=jnp.float32)  4.93 us
    all_to_all x1, starting transfers between devices, body(): lax.all_to_all(scaled, 'ep', split_axis=0, concat_axis=0, tiled=True)  4.2 us
    dot_general x1, matrix products, body(): jnp.dot(table, arrived, preferred_element_type=jnp.float32)  1.41 us
  transfers between devices with their start and end apart: 3, of which 2 were waited for; matrix products, arithmetic and copies ran while one was open for 12% of the time, Pallas kernels for 0%

commit v1 on v0

--- a/solution.py
+++ b/solution.py
@@ -1,12 +1,19 @@
+import functools
+
 import jax
 import jax.numpy as jnp
 from jax import lax
+from jax.experimental import pallas as pl
+from jax.experimental.pallas import tpu as pltpu
 from jax.sharding import PartitionSpec as P
 
 TOK_DEV = 32
-
-
-def body(hidden, down_weight, slot_gate, slot_owner, slot_row, block_count):
+LANES = 128
+VMEM_ROOM = 48 * 1024 * 1024
+MESH = pl.DeviceIdType.MESH
+
+
+def exchange_body(hidden, down_weight, slot_gate, slot_owner, slot_row, block_count):
     columns = lax.axis_size("ep")
     slot_total = hidden.shape[2]
     send = slot_total // columns
@@ -30,6 +37,199 @@
     )
 
 
+def partner(me, n, k):
+    if n & (n - 1):
+        return lax.rem(me + n - k, n), lax.rem(me + k, n)
+    other, bit = 0, 1
+    while bit < n:
+        mine = lax.rem(me // bit, 2)
+        other = other + bit * (1 - mine if k & bit else mine)
+        bit *= 2
+    return other, other
+
+
+def kernel(
+    groups, columns, send, piece,
+    hidden_ref, weight_ref, gate_ref, owner_ref, row_ref, count_ref, out_ref,
+    weight, rows_in, meta, outgoing, arrived, places,
+    weight_sem, hid_send, hid_recv, meta_send, meta_recv,
+    row_send, row_recv, place_send, place_recv,
+):
+    group, column = lax.axis_index("grp"), lax.axis_index("ep")
+    slots, width = hidden_ref.shape[2], weight_ref.shape[2]
+    pieces = width // piece
+    group_steps = list(range(1, groups))
+    column_steps = sorted(range(1, columns), key=lambda k: (k % 2, -k)) if columns > 1 else []
+
+    def weight_copy(j):
+        cols = pl.ds(j * piece, piece)
+        return pltpu.make_async_copy(
+            weight_ref.at[0, :, cols], weight.at[:, cols], weight_sem.at[j]
+        )
+
+    for j in range(pieces):
+        weight_copy(j).start()
+
+    barrier = pltpu.get_barrier_semaphore()
+    for k in group_steps:
+        pl.semaphore_signal(
+            barrier, inc=1, device_id=(partner(group, groups, k)[0], column), device_id_type=MESH
+        )
+    for k in column_steps:
+        pl.semaphore_signal(
+            barrier, inc=1, device_id=(group, partner(column, columns, k)[0]), device_id_type=MESH
+        )
+
+    lane = lax.broadcasted_iota(jnp.int32, (1, slots), 1)
+    limit = jnp.zeros((1, slots), jnp.int32)
+    for q in range(columns):
+        limit = jnp.where(lane // send == q, count_ref[0, :, q:q + 1], limit)
+    scale = jnp.where(lane % send < limit, gate_ref[0], 0.0)
+    meta[0] = jnp.zeros(meta.shape[1:], jnp.float32)
+    meta[0, 0, :, :slots] = scale
+    meta[0, 1, :, :slots] = (owner_ref[0] * TOK_DEV + row_ref[0]).astype(jnp.float32)
+    rows_in[0] = hidden_ref[0, 0]
+
+    pl.semaphore_wait(barrier, groups + columns - 2)
+
+    def hidden_copy(k):
+        return pltpu.make_async_remote_copy(
+            src_ref=hidden_ref.at[0, 0], dst_ref=rows_in.at[k],
+            send_sem=hid_send.at[k], recv_sem=hid_recv.at[k],
+            device_id=(partner(group, groups, k)[0], column), device_id_type=MESH,
+        )
+
+    def meta_copy(k):
+        return pltpu.make_async_remote_copy(
+            src_ref=meta.at[0], dst_ref=meta.at[k],
+            send_sem=meta_send.at[k], recv_sem=meta_recv.at[k],
+            device_id=(partner(group, groups, k)[0], column), device_id_type=MESH,
+        )
+
+    def row_copy(k, m):
+        to = partner(column, columns, m)[0]
+        return pltpu.make_async_remote_copy(
+            src_ref=outgoing.at[k, to], dst_ref=arrived.at[k, column],
+            send_sem=row_send.at[k, m], recv_sem=row_recv.at[k, m],
+            device_id=(group, to), device_id_type=MESH,
+        )
+
+    def place_copy(k, m):
+        return pltpu.make_async_remote_copy(
+            src_ref=meta.at[k, 1], dst_ref=places.at[k, column],
+            send_sem=place_send.at[k, m], recv_sem=place_recv.at[k, m],
+            device_id=(group, partner(column, columns, m)[0]), device_id_type=MESH,
+        )
+
+    for k in group_steps:
+        meta_copy(k).start()
+        hidden_copy(k).start()
+
+    eye = lax.broadcasted_iota(jnp.int32, (slots, slots), 0) == lax.broadcasted_iota(
+        jnp.int32, (slots, slots), 1
+    )
+    for k in range(groups):
+        if k:
+            meta_copy(k).wait_recv()
+            hidden_copy(k).wait_recv()
+        for m in column_steps:
+            place_copy(k, m).start()
+        places[k, column] = meta[k, 1]
+        factor = jnp.sum(jnp.where(eye, meta[k, 0, :, :slots], 0.0), axis=1, keepdims=True)
+        for j in range(pieces):
+            if k == 0:
+                weight_copy(j).wait()
+            cols = slice(j * piece, (j + 1) * piece)
+            product = jnp.dot(rows_in[k], weight[:, cols], preferred_element_type=jnp.float32)
+            scaled = product * factor
+            for q in range(columns):
+                outgoing[k, q, :, cols] = scaled[q * send:(q + 1) * send].astype(jnp.bfloat16)
+        for m in column_steps:
+            row_copy(k, m).start()
+        arrived[k, column] = outgoing[k, column]
+
+    total = columns * send
+    picked = lax.broadcasted_iota(jnp.int32, (meta.shape[3], total), 0) == (
+        column * send + lax.broadcasted_iota(jnp.int32, (meta.shape[3], total), 1) % send
+    )
+    picked = picked.astype(jnp.float32)
+    mine = lax.broadcasted_iota(jnp.int32, (columns, total), 0) == (
+        lax.broadcasted_iota(jnp.int32, (columns, total), 1) // send
+    )
+    wanted = (
+        group * TOK_DEV + lax.broadcasted_iota(jnp.int32, (TOK_DEV, total), 0)
+    ).astype(jnp.float32)
+    tables = []
+    for k in range(groups):
+        for m in column_steps:
+            place_copy(k, m).wait_recv()
+        index = jnp.dot(
+            places[k, :, 0], picked,
+            precision=lax.Precision.HIGHEST, preferred_element_type=jnp.float32,
+        )
+        index = jnp.sum(jnp.where(mine, index, 0.0), axis=0, keepdims=True)
+        tables.append((wanted == index).astype(jnp.bfloat16))
+    for k in range(groups):
+        for m in column_steps:
+            row_copy(k, m).wait_recv()
+    for j in range(pieces):
+        cols = slice(j * piece, (j + 1) * piece)
+        total_rows = jnp.zeros((TOK_DEV, piece), jnp.float32)
+        for k in range(groups):
+            block = jnp.concatenate([arrived[k, e, :, cols] for e in range(columns)], axis=0)
+            total_rows += jnp.dot(tables[k], block, preferred_element_type=jnp.float32)
+        out_ref[:, cols] = total_rows.astype(out_ref.dtype)
+
+    for k in group_steps:
+        meta_copy(k).wait_send()
+        hidden_copy(k).wait_send()
+    for k in range(groups):
+        for m in column_steps:
+            place_copy(k, m).wait_send()
+            row_copy(k, m).wait_send()
+
+
+def kernel_body(hidden, down_weight, slot_gate, slot_owner, slot_row, block_count):
+    groups, columns = lax.axis_size("grp"), lax.axis_size("ep")
+    slots, depth = hidden.shape[2:]
+    width = down_weight.shape[2]
+    send = slots // columns
+    lanes = -(-slots // LANES) * LANES
+    piece = 1024 if width % 1024 == 0 else width
+    vmem = pl.BlockSpec(memory_space=pltpu.VMEM)
+    dma = pltpu.SemaphoreType.DMA
+    return pl.pallas_call(
+        functools.partial(kernel, groups, columns, send, piece),
+        out_shape=jax.ShapeDtypeStruct((TOK_DEV, width), jnp.bfloat16),
+        in_specs=[vmem, pl.BlockSpec(memory_space=pl.ANY), vmem, vmem, vmem, vmem],
+        out_specs=vmem,
+        scratch_shapes=[
+            pltpu.VMEM((depth, width), jnp.bfloat16),
+            pltpu.VMEM((groups, slots, depth), jnp.bfloat16),
+            pltpu.VMEM((groups, 2, 1, lanes), jnp.float32),
+            pltpu.VMEM((groups, columns, send, width), jnp.bfloat16),
+            pltpu.VMEM((groups, columns, send, width), jnp.bfloat16),
+            pltpu.VMEM((groups, columns, 1, lanes), jnp.float32),
+            dma((width // piece,)),
+            dma((groups,)), dma((groups,)), dma((groups,)), dma((groups,)),
+            dma((groups, columns)), dma((groups, columns)),
+            dma((groups, columns)), dma((groups, columns)),
+        ],
+        compiler_params=pltpu.CompilerParams(
+            collective_id=0, has_side_effects=True, vmem_limit_bytes=56 * 1024 * 1024
+        ),
+    )(hidden, down_weight, slot_gate, slot_owner, slot_row, block_count)
+
+
+def body(hidden, down_weight, *slot_data):
+    groups, columns = lax.axis_size("grp"), lax.axis_size("ep")
+    slots, depth = hidden.shape[2:]
+    width = down_weight.shape[2]
+    held = 2 * (depth * width + groups * slots * (depth + 2 * width))
+    chosen = kernel_body if held <= VMEM_ROOM else exchange_body
+    return chosen(hidden, down_weight, *slot_data)
+
+
 def solution(mesh):
     in_specs = (
         P("grp", "ep", None, None),

time: 67 us -> 25.8 us (0.39)
  waiting for transfers between devices: 32.3 us -> 0 us
  Pallas kernels: 0 us -> 23.9 us
  between operations: 13.4 us -> 0.01 us
  starting transfers between devices: 9.44 us -> 0 us
  matrix products: 6.33 us -> 0 us
  other arithmetic: 2.09 us -> 0 us
  local copies, waits for them, and re-layouts: 3.03 us -> 1.67 us
    reduce_scatter x1 -> x0, waiting for transfers between devices: 26.8 us -> none  [body(): lax.psum_scatter(jnp.dot(table, arrived, preferred_element_type=jnp.float...]
    pallas_call x0 -> x1, Pallas kernels: none -> 23.9 us  [kernel_body(): pl.pallas_call(functools.partial(kernel, groups, columns, send, piece), o...]
    all_to_all x2 -> x0, starting transfers between devices: 9.4 us -> none  [the longest x1 5.2 us: body(): lax.all_to_all(local_index, 'ep', split_axis=0, concat_axis=0, tiled=True)]
    dot_general x2 -> x0, matrix products: 6.33 us -> none  [the longest x1 4.93 us: body(): jnp.dot(hidden[0, 0], down_weight[0], preferred_element_type=jnp.float32)]
    all_to_all x2 -> x0, waiting for transfers between devices: 5.48 us -> none  [the longest x1 5.48 us: body(): lax.all_to_all(scaled, 'ep', split_axis=0, concat_axis=0, tiled=True)]
    unnamed x2 -> x1, local copies, waits for them, and re-layouts: 0.01 us -> 1.67 us
    all_to_all x3 -> x0, local copies, waits for them, and re-layouts: 1.46 us -> none  [the longest x2 0.87 us: body(): lax.all_to_all(scaled, 'ep', split_axis=0, concat_axis=0, tiled=True)]
    broadcast_in_dim x1 -> x0, local copies, waits for them, and re-layouts: 0.72 us -> none  [body(): limits = jnp.repeat(block_count[0, 0], send)]
  transfers between devices with their start and end apart: 3 -> 0, of which waited for: 2 -> 0; matrix products, arithmetic and copies ran while one was open for 12% -> 0% of each run, Pallas kernels for 0% -> 0%
where the time goes in v1:
time: 25.8 us; the launch traced here: 25.6 us
  Pallas kernels  23.9 us (93%)
  local copies, waits for them, and re-layouts  1.67 us (6%)
    pallas_call x1, Pallas kernels, kernel_body(): pl.pallas_call(functools.partial(kernel, groups, columns, send, piece), o...  23.9 us
    unnamed x1, local copies, waits for them, and re-layouts  1.67 us

profile of v1, /device:TPU:0, one launch (start us, length us, event | category | flops | bytes accessed | tf_op | source)
XLA Modules:
  0.0 25.6 jit_solution(17102499835682598439)
XLA Ops:
  0.0 23.9 %shard_map.64 = bf16[32,4096]{1,0:T(8,128)(2,1)} custom-call(bf16[1,1,32,1024]{3,2,1,0:T(8,128)(2,1)} %hidden_ref.1, bf16[1,1024,4096]{2,1,0:T(8,128)(2,1)} %weight_ref.1, f32[1,1,32]{2,1,0:T(1,128)} %gate_ref.1, s32[1,1,32]{2,1,0:T(1,128)} %owner_ref.1, s32[1,1,32]{2,1,0:T(1,128)} %row_ref.1, s32[1,1,8]{2,1,0:T(1,128)} %count_ref.1), custom_call_target="tpu_custom_call" | custom-call | tf_op jit(solution)/shard_map/pallas_call | solution.py:201
  23.9 1.7 %copy.8 = bf16[32,4096]{1,0:T(8,128)(2,1)} copy(bf16[32,4096]{1,0:T(8,128)(2,1)} %shard_map.64) | data formatting | bytes 524288

commit v2 on v1

--- a/solution.py
+++ b/solution.py
@@ -51,8 +51,8 @@
 def kernel(
     groups, columns, send, piece,
     hidden_ref, weight_ref, gate_ref, owner_ref, row_ref, count_ref, out_ref,
-    weight, rows_in, meta, outgoing, arrived, places,
-    weight_sem, hid_send, hid_recv, meta_send, meta_recv,
+    gate, owner, row, count, result, weight, rows_in, meta, outgoing, arrived, places,
+    load_sem, store_sem, weight_sem, hid_send, hid_recv, meta_send, meta_recv,
     row_send, row_recv, place_send, place_recv,
 ):
     group, column = lax.axis_index("grp"), lax.axis_index("ep")
@@ -67,8 +67,9 @@
             weight_ref.at[0, :, cols], weight.at[:, cols], weight_sem.at[j]
         )
 
-    for j in range(pieces):
-        weight_copy(j).start()
+    def result_copy(j):
+        cols = pl.ds(j * piece, piece)
+        return pltpu.make_async_copy(result.at[:, cols], out_ref.at[:, cols], store_sem.at[j])
 
     barrier = pltpu.get_barrier_semaphore()
     for k in group_steps:
@@ -80,21 +81,34 @@
             barrier, inc=1, device_id=(group, partner(column, columns, k)[0]), device_id_type=MESH
         )
 
+    loads = [
+        pltpu.make_async_copy(gate_ref.at[0], gate, load_sem.at[0]),
+        pltpu.make_async_copy(owner_ref.at[0], owner, load_sem.at[1]),
+        pltpu.make_async_copy(row_ref.at[0], row, load_sem.at[2]),
+        pltpu.make_async_copy(count_ref.at[0], count, load_sem.at[3]),
+        pltpu.make_async_copy(hidden_ref.at[0, 0], rows_in.at[0], load_sem.at[4]),
+    ]
+    for load in loads:
+        load.start()
+    for j in range(pieces):
+        weight_copy(j).start()
+
+    for load in loads:
+        load.wait()
     lane = lax.broadcasted_iota(jnp.int32, (1, slots), 1)
     limit = jnp.zeros((1, slots), jnp.int32)
     for q in range(columns):
-        limit = jnp.where(lane // send == q, count_ref[0, :, q:q + 1], limit)
-    scale = jnp.where(lane % send < limit, gate_ref[0], 0.0)
+        limit = jnp.where(lane // send == q, count[:, q:q + 1], limit)
+    scale = jnp.where(lane % send < limit, gate[...], 0.0)
     meta[0] = jnp.zeros(meta.shape[1:], jnp.float32)
     meta[0, 0, :, :slots] = scale
-    meta[0, 1, :, :slots] = (owner_ref[0] * TOK_DEV + row_ref[0]).astype(jnp.float32)
-    rows_in[0] = hidden_ref[0, 0]
+    meta[0, 1, :, :slots] = (owner[...] * TOK_DEV + row[...]).astype(jnp.float32)
 
     pl.semaphore_wait(barrier, groups + columns - 2)
 
     def hidden_copy(k):
         return pltpu.make_async_remote_copy(
-            src_ref=hidden_ref.at[0, 0], dst_ref=rows_in.at[k],
+            src_ref=rows_in.at[0], dst_ref=rows_in.at[k],
             send_sem=hid_send.at[k], recv_sem=hid_recv.at[k],
             device_id=(partner(group, groups, k)[0], column), device_id_type=MESH,
         )
@@ -178,7 +192,8 @@
         for k in range(groups):
             block = jnp.concatenate([arrived[k, e, :, cols] for e in range(columns)], axis=0)
             total_rows += jnp.dot(tables[k], block, preferred_element_type=jnp.float32)
-        out_ref[:, cols] = total_rows.astype(out_ref.dtype)
+        result[:, cols] = total_rows.astype(out_ref.dtype)
+        result_copy(j).start()
 
     for k in group_steps:
         meta_copy(k).wait_send()
@@ -187,6 +202,8 @@
         for m in column_steps:
             place_copy(k, m).wait_send()
             row_copy(k, m).wait_send()
+    for j in range(pieces):
+        result_copy(j).wait()
 
 
 def kernel_body(hidden, down_weight, slot_gate, slot_owner, slot_row, block_count):
@@ -196,21 +213,26 @@
     send = slots // columns
     lanes = -(-slots // LANES) * LANES
     piece = 1024 if width % 1024 == 0 else width
-    vmem = pl.BlockSpec(memory_space=pltpu.VMEM)
+    hbm = pl.BlockSpec(memory_space=pltpu.HBM)
     dma = pltpu.SemaphoreType.DMA
     return pl.pallas_call(
         functools.partial(kernel, groups, columns, send, piece),
         out_shape=jax.ShapeDtypeStruct((TOK_DEV, width), jnp.bfloat16),
-        in_specs=[vmem, pl.BlockSpec(memory_space=pl.ANY), vmem, vmem, vmem, vmem],
-        out_specs=vmem,
+        in_specs=[hbm] * 6,
+        out_specs=hbm,
         scratch_shapes=[
+            pltpu.VMEM((1, slots), jnp.float32),
+            pltpu.VMEM((1, slots), jnp.int32),
+            pltpu.VMEM((1, slots), jnp.int32),
+            pltpu.VMEM((1, columns), jnp.int32),
+            pltpu.VMEM((TOK_DEV, width), jnp.bfloat16),
             pltpu.VMEM((depth, width), jnp.bfloat16),
             pltpu.VMEM((groups, slots, depth), jnp.bfloat16),
             pltpu.VMEM((groups, 2, 1, lanes), jnp.float32),
             pltpu.VMEM((groups, columns, send, width), jnp.bfloat16),
             pltpu.VMEM((groups, columns, send, width), jnp.bfloat16),
             pltpu.VMEM((groups, columns, 1, lanes), jnp.float32),
-            dma((width // piece,)),
+            dma((5,)), dma((width // piece,)), dma((width // piece,)),
             dma((groups,)), dma((groups,)), dma((groups,)), dma((groups,)),
             dma((groups, columns)), dma((groups, columns)),
             dma((groups, columns)), dma((groups, columns)),

time: 25.8 us -> 24.6 us (0.953)
  Pallas kernels: 23.9 us -> 22.7 us
    pallas_call x1, Pallas kernels: 23.9 us -> 22.7 us  [kernel_body(): pl.pallas_call(functools.partial(kernel, groups, columns, send, piece), o...]
where the time goes in v2:
time: 24.6 us; the launch traced here: 24.4 us
  Pallas kernels  22.7 us (92%)
  local copies, waits for them, and re-layouts  1.67 us (7%)
    pallas_call x1, Pallas kernels, kernel_body(): pl.pallas_call(functools.partial(kernel, groups, columns, send, piece), o...  22.7 us
    unnamed x1, local copies, waits for them, and re-layouts  1.67 us

profile of v2, /device:TPU:0, one launch (start us, length us, event | category | flops | bytes accessed | tf_op | source)
XLA Modules:
  0.0 24.4 jit_solution(9783432985848631012)
XLA Ops:
  0.0 22.7 %shard_map.64 = bf16[32,4096]{1,0:T(8,128)(2,1)} custom-call(bf16[1,1,32,1024]{3,2,1,0:T(8,128)(2,1)} %hidden_ref.1, bf16[1,1024,4096]{2,1,0:T(8,128)(2,1)} %weight_ref.1, f32[1,1,32]{2,1,0:T(1,128)} %gate_ref.1, s32[1,1,32]{2,1,0:T(1,128)} %owner_ref.1, s32[1,1,32]{2,1,0:T(1,128)} %row_ref.1, s32[1,1,8]{2,1,0:T(1,128)} %count_ref.1), custom_call_target="tpu_custom_call" | custom-call | tf_op jit(solution)/shard_map/pallas_call | solution.py:218
  22.7 1.7 %copy.8 = bf16[32,4096]{1,0:T(8,128)(2,1)} copy(bf16[32,4096]{1,0:T(8,128)(2,1)} %shard_map.64) | data formatting | bytes 524288

commit v3 on v2

--- a/solution.py
+++ b/solution.py
@@ -51,13 +51,14 @@
 def kernel(
     groups, columns, send, piece,
     hidden_ref, weight_ref, gate_ref, owner_ref, row_ref, count_ref, out_ref,
-    gate, owner, row, count, result, weight, rows_in, meta, outgoing, arrived, places,
+    gate, owner, row, count, sums, result, weight, rows_in, meta, outgoing, arrived, places,
     load_sem, store_sem, weight_sem, hid_send, hid_recv, meta_send, meta_recv,
     row_send, row_recv, place_send, place_recv,
 ):
     group, column = lax.axis_index("grp"), lax.axis_index("ep")
     slots, width = hidden_ref.shape[2], weight_ref.shape[2]
     pieces = width // piece
+    batches = [2 if k == 0 and pieces % 2 == 0 else pieces for k in range(groups)]
     group_steps = list(range(1, groups))
     column_steps = sorted(range(1, columns), key=lambda k: (k % 2, -k)) if columns > 1 else []
 
@@ -120,19 +121,36 @@
             device_id=(partner(group, groups, k)[0], column), device_id_type=MESH,
         )
 
-    def row_copy(k, m):
+    def row_copy(k, m, j):
         to = partner(column, columns, m)[0]
-        return pltpu.make_async_remote_copy(
-            src_ref=outgoing.at[k, to], dst_ref=arrived.at[k, column],
-            send_sem=row_send.at[k, m], recv_sem=row_recv.at[k, m],
+        cols = pl.ds(j * piece, batches[k] * piece)
+        return pltpu.make_async_remote_copy(
+            src_ref=outgoing.at[k, to, :, cols], dst_ref=arrived.at[k, column, :, cols],
+            send_sem=row_send.at[k], recv_sem=row_recv.at[k],
             device_id=(group, to), device_id_type=MESH,
         )
 
     def place_copy(k, m):
         return pltpu.make_async_remote_copy(
             src_ref=meta.at[k, 1], dst_ref=places.at[k, column],
-            send_sem=place_send.at[k, m], recv_sem=place_recv.at[k, m],
+            send_sem=place_send.at[k], recv_sem=place_recv.at[k],
             device_id=(group, partner(column, columns, m)[0]), device_id_type=MESH,
+        )
+
+    def all_rows(k):
+        return pltpu.make_async_remote_copy(
+            src_ref=outgoing.at[k, pl.ds(0, columns - 1)],
+            dst_ref=arrived.at[k, pl.ds(0, columns - 1)],
+            send_sem=row_send.at[k], recv_sem=row_recv.at[k],
+            device_id=(group, partner(column, columns, 1)[0]), device_id_type=MESH,
+        )
+
+    def all_places(k):
+        return pltpu.make_async_remote_copy(
+            src_ref=places.at[k, pl.ds(0, columns - 1)],
+            dst_ref=places.at[k, pl.ds(0, columns - 1)],
+            send_sem=place_send.at[k], recv_sem=place_recv.at[k],
+            device_id=(group, partner(column, columns, 1)[0]), device_id_type=MESH,
         )
 
     for k in group_steps:
@@ -158,8 +176,9 @@
             scaled = product * factor
             for q in range(columns):
                 outgoing[k, q, :, cols] = scaled[q * send:(q + 1) * send].astype(jnp.bfloat16)
-        for m in column_steps:
-            row_copy(k, m).start()
+            if (j + 1) % batches[k] == 0:
+                for m in column_steps:
+                    row_copy(k, m, j + 1 - batches[k]).start()
         arrived[k, column] = outgoing[k, column]
 
     total = columns * send
@@ -175,8 +194,8 @@
     ).astype(jnp.float32)
     tables = []
     for k in range(groups):
-        for m in column_steps:
-            place_copy(k, m).wait_recv()
+        if column_steps:
+            all_places(k).wait_recv()
         index = jnp.dot(
             places[k, :, 0], picked,
             precision=lax.Precision.HIGHEST, preferred_element_type=jnp.float32,
@@ -184,24 +203,27 @@
         index = jnp.sum(jnp.where(mine, index, 0.0), axis=0, keepdims=True)
         tables.append((wanted == index).astype(jnp.bfloat16))
     for k in range(groups):
-        for m in column_steps:
-            row_copy(k, m).wait_recv()
-    for j in range(pieces):
-        cols = slice(j * piece, (j + 1) * piece)
-        total_rows = jnp.zeros((TOK_DEV, piece), jnp.float32)
-        for k in range(groups):
+        if column_steps:
+            all_rows(k).wait_recv()
+        for j in range(pieces):
+            cols = slice(j * piece, (j + 1) * piece)
             block = jnp.concatenate([arrived[k, e, :, cols] for e in range(columns)], axis=0)
-            total_rows += jnp.dot(tables[k], block, preferred_element_type=jnp.float32)
-        result[:, cols] = total_rows.astype(out_ref.dtype)
-        result_copy(j).start()
+            rows = jnp.dot(tables[k], block, preferred_element_type=jnp.float32)
+            if k:
+                rows = sums[:, cols] + rows
+            if k < groups - 1:
+                sums[:, cols] = rows
+            else:
+                result[:, cols] = rows.astype(out_ref.dtype)
+                result_copy(j).start()
 
     for k in group_steps:
         meta_copy(k).wait_send()
         hidden_copy(k).wait_send()
     for k in range(groups):
-        for m in column_steps:
-            place_copy(k, m).wait_send()
-            row_copy(k, m).wait_send()
+        if column_steps:
+            all_places(k).wait_send()
+            all_rows(k).wait_send()
     for j in range(pieces):
         result_copy(j).wait()
 
@@ -225,6 +247,7 @@
             pltpu.VMEM((1, slots), jnp.int32),
             pltpu.VMEM((1, slots), jnp.int32),
             pltpu.VMEM((1, columns), jnp.int32),
+            pltpu.VMEM((TOK_DEV, width), jnp.float32),
             pltpu.VMEM((TOK_DEV, width), jnp.bfloat16),
             pltpu.VMEM((depth, width), jnp.bfloat16),
             pltpu.VMEM((groups, slots, depth), jnp.bfloat16),
@@ -234,8 +257,7 @@
             pltpu.VMEM((groups, columns, 1, lanes), jnp.float32),
             dma((5,)), dma((width // piece,)), dma((width // piece,)),
             dma((groups,)), dma((groups,)), dma((groups,)), dma((groups,)),
-            dma((groups, columns)), dma((groups, columns)),
-            dma((groups, columns)), dma((groups, columns)),
+            dma((groups,)), dma((groups,)), dma((groups,)), dma((groups,)),
         ],
         compiler_params=pltpu.CompilerParams(
             collective_id=0, has_side_effects=True, vmem_limit_bytes=56 * 1024 * 1024

time: 24.6 us -> 23.1 us (0.939)
  Pallas kernels: 22.7 us -> 21.3 us
    pallas_call x1, Pallas kernels: 22.7 us -> 21.3 us  [kernel_body(): pl.pallas_call(functools.partial(kernel, groups, columns, send, piece), o...]
where the time goes in v3:
time: 23.1 us; the launch traced here: 22.9 us
  Pallas kernels  21.3 us (92%)
  local copies, waits for them, and re-layouts  1.67 us (7%)
    pallas_call x1, Pallas kernels, kernel_body(): pl.pallas_call(functools.partial(kernel, groups, columns, send, piece), o...  21.3 us
    unnamed x1, local copies, waits for them, and re-layouts  1.67 us

profile of v3, /device:TPU:0, one launch (start us, length us, event | category | flops | bytes accessed | tf_op | source)
XLA Modules:
  0.0 22.9 jit_solution(5214745632213083028)
XLA Ops:
  0.0 21.3 %shard_map.64 = bf16[32,4096]{1,0:T(8,128)(2,1)} custom-call(bf16[1,1,32,1024]{3,2,1,0:T(8,128)(2,1)} %hidden_ref.1, bf16[1,1024,4096]{2,1,0:T(8,128)(2,1)} %weight_ref.1, f32[1,1,32]{2,1,0:T(1,128)} %gate_ref.1, s32[1,1,32]{2,1,0:T(1,128)} %owner_ref.1, s32[1,1,32]{2,1,0:T(1,128)} %row_ref.1, s32[1,1,8]{2,1,0:T(1,128)} %count_ref.1), custom_call_target="tpu_custom_call" | custom-call | tf_op jit(solution)/shard_map/pallas_call | solution.py:240
  21.3 1.7 %copy.8 = bf16[32,4096]{1,0:T(8,128)(2,1)} copy(bf16[32,4096]{1,0:T(8,128)(2,1)} %shard_map.64) | data formatting | bytes 524288
